TPU v7x, 32 devices: a whole 2x2x4 slice. The times are simulated.
32 devices in a mesh: dp: 8 (over z, y), tensor: 4 (over x, core).
Axes of the slice: x: 2, y: 2, z: 4, core: 2. Of those that a mesh axis runs over, the one named last changes fastest.
Arguments:
- hidden_in: bfloat16 [16384, 768], P(('dp', 'tensor')), may hold values from -6 to 6
- lengths: int32 [16], P('dp'), may hold values from 1 to 1024, as said below
- ln1_gain: float32 [768], replicated, may hold values from 0.5 to 1.5
- ln1_shift: float32 [768], replicated, may hold values from -1.75 to 1.75
- qkv_weight: bfloat16 [3, 768, 768], P(None, None, 'tensor'), may hold values from -0.21875 to 0.21875
- qv_bias: float32 [2, 768], P(None, 'tensor'), may hold values from -3 to 3
- out_weight: bfloat16 [768, 768], P('tensor'), may hold values from -1.75 to 1.75
- out_bias: float32 [768], replicated, may hold values from -1.75 to 1.75
- ln2_gain: float32 [768], replicated, may hold values from 0.5 to 1.5
- ln2_shift: float32 [768], replicated, may hold values from -1.75 to 1.75
- up_weight: bfloat16 [768, 3072], P(None, 'tensor'), may hold values from -0.21875 to 0.21875
- up_bias: bfloat16 [3072], P('tensor'), may hold values from -3 to 3
- down_weight: bfloat16 [3072, 768], P('tensor'), may hold values from -0.109375 to 0.109375
- down_bias: float32 [768], replicated, may hold values from -1.75 to 1.75
- out_grad: bfloat16 [16384, 768], P(('dp', 'tensor')), may hold values from -6 to 6
Outputs:
- output: bfloat16 [16384, 768], P(('dp', 'tensor'))
- input_grad: bfloat16 [16384, 768], P(('dp', 'tensor'))
- ln1_gain_grad: float32 [768], replicated
- ln1_shift_grad: float32 [768], replicated
- qkv_weight_grad: float32 [3, 768, 768], P(None, None, 'tensor')
- qv_bias_grad: float32 [2, 768], P(None, 'tensor')
- out_weight_grad: float32 [768, 768], P('tensor')
- out_bias_grad: float32 [768], replicated
- ln2_gain_grad: float32 [768], replicated
- ln2_shift_grad: float32 [768], replicated
- up_weight_grad: float32 [768, 3072], P(None, 'tensor')
- up_bias_grad: float32 [3072], P('tensor')
- down_weight_grad: float32 [3072, 768], P('tensor')
- down_bias_grad: float32 [768], replicated
Inputs may be any that keep to these rules, and one draw needn't show every extreme that they name: `lengths`: some slot's length is exactly 1024.
All inputs are finite; a program needn't handle non-finite values.
Results may differ from a plain program's by a relative error of at most 0.012.
The roundings to bfloat16 on the way count: a program that leaves them out, or rounds other values in their place, can miss the bound.
Values may be sent and summed in bfloat16 or wider, within the bound.
A program may use at most 192 MiB of HBM per device.

v0:
```python
import math

import jax
import jax.numpy as jnp
from jax import lax
from jax.experimental import pallas as pl
from jax.experimental.pallas import tpu as pltpu
from jax.sharding import PartitionSpec as P

HD = 64
BLK = 256
BIG = 1e30
sel_factor = 4.0
score_scale = 1.0 / math.sqrt(HD)
f32 = jnp.float32
bf16 = jnp.bfloat16


def mm(a, b):
    return lax.dot_general(a, b, (((1,), (0,)), ((), ())), preferred_element_type=f32)


def mm_nt(a, b):
    return lax.dot_general(a, b, (((1,), (1,)), ((), ())), preferred_element_type=f32)


def flip(a):
    return a.astype(f32).T.astype(bf16)


def split_mm(tri, x):
    hi = x.astype(bf16)
    lo = (x - hi.astype(f32)).astype(bf16)
    return mm(tri, hi) + mm(tri, lo)


def head_mask(h, width):
    return lax.broadcasted_iota(jnp.int32, (BLK, width), 1) // HD == h


def masked_rows(x, mask, scale):
    return jnp.where(mask, x.astype(f32) * scale, 0.0).astype(bf16)


def fwd_block(i, heads, first, q_ref, k_ref, v_ref, fence, o_ref, lse_ref):
    width = q_ref.shape[1]
    cols = (i + 1) * BLK
    keys = k_ref[:cols, :]
    vals = v_ref[:cols, :]
    fenced = fence[:, :cols]
    lane = lax.broadcasted_iota(jnp.int32, (BLK, 128), 1)
    lse_ref[...] = jnp.zeros_like(lse_ref)
    out_scr = first

    def head(h, _):
        mask = head_mask(h, width)
        s = mm_nt(masked_rows(q_ref[...], mask, score_scale), keys) - fenced
        top = jnp.max(s, -1, keepdims=True)
        e = jnp.exp(s - top)
        total = jnp.sum(e, -1, keepdims=True)
        p = (e * (1.0 / total)).astype(bf16)
        out = mm(p, vals)
        out_scr[...] = jnp.where(mask, out, out_scr[...])
        lse_ref[...] = jnp.where(lane == h, top + jnp.log(total), lse_ref[...])
        return 0

    lax.fori_loop(0, heads, head, 0)
    o_ref[...] = out_scr[...].astype(bf16)


def make_fence(i, seq_len, length, sq_ref, sk_ref, fence, carry):
    cols = (i + 1) * BLK
    s0 = mm_nt(sq_ref[...], sk_ref[:cols, :]) * score_scale
    row = i * BLK + lax.broadcasted_iota(jnp.int32, (BLK, cols), 0)
    col = lax.broadcasted_iota(jnp.int32, (BLK, cols), 1)
    picked = (col >= 1) & (col < row)
    sel = jnp.where(picked, jnp.maximum(s0, 0.0), 0.0) * (sel_factor / seq_len)
    r2 = lax.broadcasted_iota(jnp.int32, (BLK, BLK), 0)
    c2 = lax.broadcasted_iota(jnp.int32, (BLK, BLK), 1)
    tri = jnp.where(c2 < r2, 1.0, 0.0).astype(bf16)
    total = carry[0:1, :cols] + split_mm(tri, sel)
    carry[0:1, :cols] = total[BLK - 1 : BLK, :] + sel[BLK - 1 : BLK, :]
    fence[:, :cols] = jnp.where((col <= row) & (col < length), total, BIG)


def bwd_block(i, heads, q_ref, k_ref, v_ref, do_ref, lse_ref, f_ref, sq_ref, sk_ref,
              dq_ref, dsq_ref, dq_scr, dkt, dvt, dskt, later, fsum, qt, dot_):
    width = q_ref.shape[1]
    seq_len = k_ref.shape[0]
    cols = (i + 1) * BLK
    keys = k_ref[:cols, :]
    vals = v_ref[:cols, :]
    lane = lax.broadcasted_iota(jnp.int32, (BLK, 128), 1)
    qt[...] = (q_ref[...].astype(f32) * score_scale).T.astype(bf16)
    dot_[...] = flip(do_ref[...])
    fsum[:, :cols] = jnp.zeros((BLK, cols), f32)

    def head(h, _):
        mask = head_mask(h, width)
        lse = jnp.sum(jnp.where(lane == h, lse_ref[...], 0.0), -1, keepdims=True)
        s = mm_nt(masked_rows(q_ref[...], mask, score_scale), keys)
        p = jnp.exp(s - f_ref[:, :cols] - lse)
        dp = mm_nt(masked_rows(do_ref[...], mask, 1.0), vals)
        delta = jnp.sum(p * dp, -1, keepdims=True)
        g = (p * (dp - delta)).astype(bf16)
        rows = pl.ds(pl.multiple_of(h * HD, HD), HD)
        dq_scr[...] = jnp.where(mask, mm(g, keys), dq_scr[...])
        dkt[rows, :cols] += mm(qt[rows, :], g)
        dvt[rows, :cols] += mm(dot_[rows, :], p.astype(bf16))
        fsum[:, :cols] += g.astype(f32)
        return 0

    lax.fori_loop(0, heads, head, 0, unroll=True)
    dq_ref[...] = (dq_scr[...] * score_scale).astype(bf16)
    grad = -fsum[:, :cols]
    r2 = lax.broadcasted_iota(jnp.int32, (BLK, BLK), 0)
    c2 = lax.broadcasted_iota(jnp.int32, (BLK, BLK), 1)
    tri = jnp.where(c2 > r2, 1.0, 0.0).astype(bf16)
    dsel = later[0:1, :cols] + split_mm(tri, grad)
    later[0:1, :cols] = dsel[0:1, :] + grad[0:1, :]
    s0 = mm_nt(sq_ref[...], sk_ref[:cols, :])
    row = i * BLK + lax.broadcasted_iota(jnp.int32, (BLK, cols), 0)
    col = lax.broadcasted_iota(jnp.int32, (BLK, cols), 1)
    keep = (col >= 1) & (col < row) & (s0 > 0)
    gsel = jnp.where(keep, dsel * (sel_factor / seq_len), 0.0).astype(bf16)
    dsq_ref[...] = mm(gsel, sk_ref[:cols, :]) * score_scale
    sqt = (sq_ref[...].astype(f32) * score_scale).T.astype(bf16)
    dskt[:, :cols] += mm(sqt, gsel)


epsilon = 1e-05


def mm_tn(a, b):
    return lax.dot_general(a, b, (((0,), (0,)), ((), ())), preferred_element_type=f32)


def send(src, dst, send_sem, recv_sem, **where):
    copy = pltpu.make_async_remote_copy(
        src_ref=src,
        dst_ref=dst,
        send_sem=send_sem,
        recv_sem=recv_sem,
        device_id=where,
        device_id_type=pl.DeviceIdType.MESH,
    )
    copy.start()
    return copy


def meet(devices):
    barrier = pltpu.get_barrier_semaphore()
    for where in devices:
        pl.semaphore_signal(barrier, inc=1, device_id=where, device_id_type=pl.DeviceIdType.MESH)
    pl.semaphore_wait(barrier, len(devices))


def norm_parts(x):
    centre = x - jnp.mean(x, -1, keepdims=True)
    r = lax.rsqrt(jnp.mean(centre * centre, -1, keepdims=True) + epsilon)
    return centre * r, r


def norm_back(e, xhat, r):
    return r * (e - jnp.mean(e, -1, keepdims=True) - xhat * jnp.mean(e * xhat, -1, keepdims=True))


def gelu_pair(u):
    k = math.sqrt(2.0 / math.pi)
    square = u * u
    t = jnp.tanh(k * u * (1.0 + 0.044715 * square))
    act = 0.5 * u * (1.0 + t)
    slope = 0.5 * (1.0 + t) + 0.5 * u * (1.0 - t * t) * (k * (1.0 + 3.0 * 0.044715 * square))
    return act, slope


def feed_kernel(
    o1, o2, wo1, wo2, hidden, g0, g1, g2, g3, vecs, up, down,
    rows_out, gmid, partial, branch_x, up_g, down_g, sums,
    inner, gs, act, gpre, mid, attn_send, attn_recv,
    near_send, near_recv, far_send, far_recv, x_send, x_recv,
    bn_send, bn_recv, bf_send, bf_recv, gin,
    g_sem, a_s, a_r, i_s, i_r, x_s, x_r, f_s, f_r, n_s, n_r, c_s, c_r, r_s, r_r, b_s, b_r, o_s, o_r,
):
    me = lax.axis_index("tensor")
    odd = lax.rem(me, 2)
    core = me + 1 - 2 * odd
    far = lax.rem(me + 2, 4)
    rows = hidden.shape[0]
    pieces = rows // BLK
    loads = [pltpu.make_async_copy(g, gs.at[i], g_sem.at[i]) for i, g in enumerate((g0, g1, g2, g3))]
    for c in loads:
        c.start()
    meet([{"tensor": core}, {"tensor": far}])
    out_bias, gain, shift, down_bias, up_bias = (vecs[j : j + 1, :] for j in range(5))

    def attn(start):
        part = pl.ds(pl.multiple_of(start, BLK), BLK)
        return mm(o1[part, :], wo1[...]) + mm(o2[part, :], wo2[...])

    sends = []
    attn_copies = []
    for c in range(pieces):
        here = pl.ds(c * BLK, BLK)
        attn_send[here, :] = attn((1 - odd) * rows + c * BLK).astype(bf16)
        attn_copies.append(send(attn_send.at[here], attn_recv.at[here], a_s.at[c], a_r.at[c], tensor=core))
    inner_copies, far_copies = [], []
    for c in range(pieces):
        here = pl.ds(c * BLK, BLK)
        mine = attn(odd * rows + c * BLK)
        attn_copies[c].wait_recv()
        m = hidden[here, :].astype(f32) + (mine + attn_recv[here, :].astype(f32)) + out_bias
        mid[here, :] = m
        xhat, r = norm_parts(m)
        inner[0, here, :] = (xhat * gain + shift).astype(bf16)
        far_copies.append(send(inner.at[0, here], inner.at[2, here], x_s.at[c], x_r.at[c], tensor=far))
        inner_copies.append(send(inner.at[0, here], inner.at[1, here], i_s.at[c], i_r.at[c], tensor=core))
    sends += attn_copies + inner_copies + far_copies
    for c in loads:
        c.wait()
    sums[...] = jnp.zeros_like(sums)

    def feed(slot, start):
        part = pl.ds(pl.multiple_of(start, BLK), BLK)
        pre = mm(inner[slot, part, :], up[...]) + up_bias
        a, slope = gelu_pair(pre)
        act[slot, part, :] = a.astype(bf16)
        gp = (mm_nt(gs[slot, part, :], down[...]) * slope).astype(bf16)
        gpre[slot, part, :] = gp
        sums[4:5, :] += jnp.sum(gp.astype(f32), 0, keepdims=True)

    def near(i, _):
        @pl.when(i == pieces)
        def _():
            for c in inner_copies:
                c.wait_recv()

        feed(i // pieces, lax.rem(i, pieces) * BLK)
        return 0

    lax.fori_loop(0, 2 * pieces, near, 0)

    def near_other(c, _):
        part = pl.ds(pl.multiple_of(c * BLK, BLK), BLK)
        near_send[part, :] = mm_nt(gpre[1, part, :], up[...]).astype(bf16)
        bn_send[part, :] = mm(act[1, part, :], down[...]).astype(bf16)
        return 0

    lax.fori_loop(0, pieces, near_other, 0)
    near_copy = send(near_send, near_recv, n_s.at[0], n_r.at[0], tensor=core)
    branch_copy = send(bn_send, bn_recv, n_s.at[1], n_r.at[1], tensor=core)

    def near_own(c, _):
        part = pl.ds(pl.multiple_of(c * BLK, BLK), BLK)
        gin[part, :] = mm_nt(gpre[0, part, :], up[...])
        partial[part, :] = mid[part, :] + mm(act[0, part, :], down[...]) + down_bias
        return 0

    lax.fori_loop(0, pieces, near_own, 0)

    def plan(src, dst, c, send_sem, recv_sem, where):
        here = pl.ds(pl.multiple_of(c * BLK, BLK), BLK)
        return pltpu.make_async_remote_copy(
            src_ref=src.at[here], dst_ref=dst.at[here], send_sem=send_sem.at[c],
            recv_sem=recv_sem.at[c], device_id={"tensor": where},
            device_id_type=pl.DeviceIdType.MESH,
        )

    def arrive(c):
        return plan(inner.at[0], inner.at[2], c, x_s, x_r, far)

    def hand_on(c):
        return plan(inner.at[2], inner.at[3], c, f_s, f_r, core)

    def crossed(c):
        return plan(far_send, far_recv, c, c_s, c_r, core)

    def back(c):
        return plan(x_send, x_recv, c, r_s, r_r, far)

    depth = up.shape[0]
    if up_g.shape[0] > depth:
        up_g[depth:, :] = jnp.zeros((up_g.shape[0] - depth, up_g.shape[1]), bf16)
        down_g[depth:, :] = jnp.zeros((up_g.shape[0] - depth, up_g.shape[1]), bf16)

    def weights(left, right, out):
        def tile(j, _):
            part = pl.ds(pl.multiple_of(j * BLK, BLK), BLK)
            total = mm_tn(left[0, :, part], right[0])
            for k in range(1, 4):
                total = total + mm_tn(left[k, :, part], right[k])
            out[part, :] = total.astype(bf16)
            return 0

        lax.fori_loop(0, depth // BLK, tile, 0)

    def far_step(i, _):
        c = i // 2
        which = lax.rem(i, 2)
        here = pl.ds(pl.multiple_of(c * BLK, BLK), BLK)

        @pl.when(which == 0)
        def _():
            arrive(c).wait_recv()
            hand_on(c).start()

        @pl.when(which == 1)
        def _():
            hand_on(c).wait_recv()

        feed(2 + which, c * BLK)

        @pl.when(which == 1)
        def _():
            far_send[here, :] = mm_nt(gpre[3, here, :], up[...]).astype(bf16)
            crossed(c).start()
            g = mm_nt(gpre[2, here, :], up[...])
            crossed(c).wait_recv()
            x_send[here, :] = (g + far_recv[here, :].astype(f32)).astype(bf16)
            back(c).start()

        return 0

    lax.fori_loop(0, 2 * pieces, far_step, 0)

    def far_out(c, _):
        here = pl.ds(pl.multiple_of(c * BLK, BLK), BLK)
        bf_send[here, :] = mm(act[3, here, :], down[...]).astype(bf16)
        return 0

    lax.fori_loop(0, pieces, far_out, 0)
    far_branch = send(bf_send, bf_recv, b_s, b_r, tensor=core)
    weights(inner, gpre, up_g)
    weights(act, gs, down_g)
    far_branch.wait_recv()
    for c in range(pieces):
        here = pl.ds(c * BLK, BLK)
        b = mm(act[2, here, :], down[...])
        branch_x[here, :] = (b + bf_recv[here, :].astype(f32)).astype(bf16)
    near_copy.wait_recv()
    branch_copy.wait_recv()
    partial[...] += bn_recv[...].astype(f32)
    rows_copies = []
    for c in range(pieces):
        here = pl.ds(c * BLK, BLK)
        xhat, r = norm_parts(mid[here, :])
        back(c).wait_recv()
        g = gin[here, :] + near_recv[here, :].astype(f32) + x_recv[here, :].astype(f32)
        g_out = gs[0, here, :].astype(f32)
        gm = g_out + norm_back(g * gain, xhat, r)
        gmid[here, :] = gm
        there = pl.ds(pl.multiple_of(odd * rows + c * BLK, BLK), BLK)
        ga = gm.astype(bf16)
        rows_out[there, :] = ga
        rows_copies.append(
            send(rows_out.at[there], rows_out.at[there], o_s.at[c], o_r.at[c], tensor=core)
        )
        sums[0:1, :] += jnp.sum(g * xhat, 0, keepdims=True)
        sums[1:2, :] += jnp.sum(g, 0, keepdims=True)
        sums[2:3, :] += jnp.sum(ga.astype(f32), 0, keepdims=True)
        sums[3:4, :] += jnp.sum(g_out, 0, keepdims=True)
    for c in rows_copies:
        c.wait_recv()
    for c in range(pieces):
        sends += [hand_on(c), crossed(c), back(c)]
    for c in sends + rows_copies + [near_copy, branch_copy, far_branch]:
        c.wait_send()


def feed_forward(padded, o1, o2, wo1, wo2, hidden, gs, vecs, up, down):
    rows, depth = hidden.shape
    width = up.shape[1]
    pieces = rows // BLK
    vmem = pl.BlockSpec(memory_space=pltpu.VMEM)
    anyw = pl.BlockSpec(memory_space=pl.ANY)
    dma = pltpu.SemaphoreType.DMA
    wide = pltpu.VMEM((rows, depth), bf16)
    each = [dma((pieces,))] * 2
    return pl.pallas_call(
        feed_kernel,
        in_specs=[vmem] * 5 + [anyw] * 4 + [vmem] * 3,
        out_specs=[vmem] * 7,
        out_shape=[
            jax.ShapeDtypeStruct((2 * rows, depth), bf16),
            jax.ShapeDtypeStruct((rows, depth), f32),
            jax.ShapeDtypeStruct((rows, depth), f32),
            jax.ShapeDtypeStruct((rows, depth), bf16),
            jax.ShapeDtypeStruct((padded, width), bf16),
            jax.ShapeDtypeStruct((padded, width), bf16),
            jax.ShapeDtypeStruct((8, depth), f32),
        ],
        scratch_shapes=[
            pltpu.VMEM((4, rows, depth), bf16),
            pltpu.VMEM((4, rows, depth), bf16),
            pltpu.VMEM((4, rows, width), bf16),
            pltpu.VMEM((4, rows, width), bf16),
            pltpu.VMEM((rows, depth), f32),
            wide, wide, wide, wide, wide, wide, wide, wide, wide, wide, wide, wide,
            pltpu.VMEM((rows, depth), f32),
            dma((4,)),
            *each, *each, *each, *each,
            dma((2,)), dma((2,)),
            *each, *each,
            dma, dma,
            *each,
        ],
        compiler_params=pltpu.CompilerParams(
            collective_id=1, has_side_effects=True, vmem_limit_bytes=62 * 1024 * 1024
        ),
        name="feed_forward",
    )(o1, o2, wo1, wo2, hidden, *gs, vecs, up, down)

def back_kernel(n, chunk, piece, depth, lengths, up_h, down_h, branch_x, *rest):
    held, outs = rest[:LOADS], rest[LOADS : LOADS + 7]
    back_body(n, chunk, piece, depth, lengths, up_h, down_h, branch_x, held, outs, *rest[LOADS + 7 :])


LOADS = 27


def back_body(
    n, chunk, piece, depth, lengths, up_h, down_h, branch_x, held, outs,
    up_g, up_recv, rows_in, os, wo, qkv, lse, fence, sq, sk, normed, down_g, w, sel_w,
    hidden, gmid, vecs, sums, partial, ld_s,
    go, grads, dsums,
    dq_scr, dkt, dvt, dskt, later, fsum, qt, dot_,
    dsel, ng_send, ng_recv, ng_own, far_s, far_r, faro_s, faro_r, gb, ga,
    yd, yb, ya, ys, su, sd, sb, sa, ss, zu, zd, zb, za, zs,
    ts, small, out_s, bx_recv, sel_mine, sel_core, sel_far,
    core_s, core_r, f_s, f_r, sl_s, sl_r, y_s, y_r, z_s, z_r, t_s, t_r, az_s, az_r, ay_s, ay_r,
):
    fu, fd, fb, fa, small_out, input_grad, output = outs
    places = (
        up_g, rows_in, os.at[0], wo.at[0], qkv.at[0, 0], qkv.at[0, 1], qkv.at[0, 2],
        lse.at[0], fence, sq, sk, normed, down_g, wo.at[1], qkv.at[1, 0], qkv.at[1, 1],
        qkv.at[1, 2], lse.at[1], w.at[0], w.at[1], sel_w, os.at[1], hidden, gmid, vecs, sums, partial,
    )
    idx = lax.axis_index("dp")
    par = lax.rem(idx, 2)
    m = n // 2
    own = pl.ds(pl.multiple_of(par * m * chunk, m * chunk), m * chunk)
    loads = [
        pltpu.make_async_copy(h.at[own] if j in (0, 12) else h, v, ld_s.at[j])
        for j, (h, v) in enumerate(zip(held, places))
    ]
    for c in loads:
        c.start()

    def need(*which):
        for j in which:
            loads[j].wait()

    me = lax.axis_index("tensor")
    odd = lax.rem(me, 2)
    z = lax.div(idx, 2)
    rows = hidden.shape[0]
    seq_len = normed.shape[0]
    width = wo.shape[1]
    heads = width // HD
    ranks = 4
    core = me + 1 - 2 * odd
    far = lax.rem(me + 2, ranks)
    ydev = idx + 1 - 2 * par
    peers = [lax.rem(me + d, ranks) for d in range(1, ranks)]
    mates = []
    for b in range(m.bit_length() - 1):
        bit = lax.rem(lax.div(z, 1 << b), 2)
        mates.append(z + (1 - 2 * bit) * (1 << b))
    length = jnp.where(me < 2, lengths[0], lengths[1])
    meet(
        [{"tensor": p} for p in peers]
        + [{"dp": ydev}]
        + [{"dp": 2 * p + par} for p in mates]
    )
    at = par * m + z
    source = (gb, ga, small, up_g, down_g)
    yrecv = (yb, ya, ys, up_recv, yd)
    ysum = (sb, sa, ss, su, sd)
    zrecv = (zb, za, zs, zu, zd)
    full = (fb, fa, out_s, fu, fd)
    size = (gb.shape[0] // n, ga.shape[0] // n, piece, chunk, chunk)

    def plan(src, dst, send_sem, recv_sem, **where):
        return pltpu.make_async_remote_copy(
            src_ref=src, dst_ref=dst, send_sem=send_sem, recv_sem=recv_sem,
            device_id=where, device_id_type=pl.DeviceIdType.MESH,
        )

    def block(start, k):
        return pl.ds(pl.multiple_of(start * size[k], size[k]), size[k])

    def y_copy(k):
        half = m * size[k]
        give = pl.ds(pl.multiple_of((1 - par) * half, half), half)
        src = {3: up_h, 4: down_h}.get(k, source[k])
        return plan(src.at[give], yrecv[k], y_s.at[k], y_r.at[k], dp=ydev)

    bits = m.bit_length() - 1
    first_slot = [0]
    for b in range(bits):
        first_slot.append(first_slot[-1] + (m >> (b + 1)))

    def held_chunk(who, b, j):
        return lax.rem(who, 2 << b) + j * (2 << b)

    def mate(b):
        return mates[b]

    def z_copy(k, b, j):
        slot = first_slot[b] + j
        return plan(
            ysum[k].at[block(held_chunk(mate(b), b, j), k)], zrecv[k].at[slot],
            z_s.at[k, slot], z_r.at[k, slot], dp=2 * mate(b) + par,
        )

    def az_copy(k, b, j):
        slot = first_slot[b] + j
        mine = full[k].at[block(par * m + held_chunk(z, b, j), k)]
        return plan(mine, mine, az_s.at[k, slot], az_r.at[k, slot], dp=2 * mate(b) + par)

    def ay_copy(k, b, j):
        chunk_id, slot = (z, m - 1) if b is None else (held_chunk(mate(b), b, j), first_slot[b] + j)
        came = full[k].at[block(par * m + chunk_id, k)]
        return plan(came, came, ay_s.at[k, slot], ay_r.at[k, slot], dp=ydev)

    def stage(b):
        return range(m >> (b + 1))

    def z_start(k, b):
        for j in stage(b):
            z_copy(k, b, j).start()

    def y_finish(k):
        half = m * size[k]
        keep = pl.ds(pl.multiple_of(par * half, half), half)
        y_copy(k).wait_recv()
        mine = source[k][...] if k > 2 else source[k][keep, :]
        total = mine.astype(f32) + yrecv[k][...].astype(f32)
        ysum[k][...] = total.astype(ysum[k].dtype)
        z_start(k, 0)

    def z_next(k, b):
        for j in stage(b):
            z_copy(k, b, j).wait_recv()
            here = block(held_chunk(z, b, j), k)
            total = ysum[k][here, :].astype(f32) + zrecv[k][first_slot[b] + j].astype(f32)
            ysum[k][here, :] = total.astype(ysum[k].dtype)
        z_start(k, b + 1)

    def z_finish(k):
        for b in range(1, bits - 1):
            z_next(k, b)
        z_copy(k, bits - 1, 0).wait_recv()
        return ysum[k][block(z, k), :].astype(f32) + zrecv[k][first_slot[bits - 1]].astype(f32)

    def az_start(k, b):
        for j in stage(b):
            az_copy(k, b, j).start()

    def spread(k):
        az_start(k, bits - 1)
        ay_copy(k, None, 0).start()

    def forward(k, b):
        for j in stage(b):
            az_copy(k, b, j).wait_recv()
        if b > 0:
            az_start(k, b - 1)
        for j in stage(b):
            ay_copy(k, b, j).start()

    def forward_early(k):
        for b in reversed(range(1, bits)):
            forward(k, b)

    def far_copy(j):
        part = pl.ds(pl.multiple_of(j * width, width), width)
        return plan(far_s.at[part], far_r.at[part], f_s.at[2 + j], f_r.at[2 + j], tensor=far)

    out_copy = plan(faro_s, faro_r, f_s.at[0], f_r.at[0], tensor=far)
    branch_copy = plan(branch_x, bx_recv, f_s.at[1], f_r.at[1], tensor=far)
    core_copy = plan(ng_send, ng_recv, core_s, core_r, tensor=core)
    to_core = plan(sel_mine, sel_core, sl_s.at[0], sl_r.at[0], tensor=core)
    to_first = plan(sel_mine, sel_far, sl_s.at[1], sl_r.at[1], tensor=far)

    y_copy(3).start()
    y_copy(4).start()
    need(*range(13))

    def hook(g, i):
        if i == 1:

            @pl.when(g == 0)
            def _():
                y_finish(3)

            @pl.when(g == 1)
            def _():
                fu[block(at, 3), :] = z_finish(3).astype(bf16)
                spread(3)
                z_next(4, 0)

        if i == seq_len // BLK - 1:

            @pl.when(g == 1)
            def _():
                z_next(3, 0)
                y_finish(4)

    def group(g, _):
        @pl.when(g == 1)
        def _():
            need(*range(13, 18), 21)

        total = mm_tn(os[g], rows_in[...])

        @pl.when(g == 0)
        def _():
            faro_s[...] = total.astype(bf16)
            out_copy.start()

        @pl.when(g == 1)
        def _():
            out_copy.wait_recv()
            ga[width : 2 * width, :] = (total + faro_r[...].astype(f32)).astype(bf16)

        def head_grad(j, _):
            here = pl.ds(pl.multiple_of(j * BLK, BLK), BLK)
            go[here, :] = mm_nt(rows_in[here, :], wo[g]).astype(bf16)
            return 0

        lax.fori_loop(0, seq_len // BLK, head_grad, 0)
        for r in (dkt, dvt, dskt, later):
            r[...] = jnp.zeros_like(r)
        for i in reversed(range(seq_len // BLK)):
            here = pl.ds(i * BLK, BLK)
            bwd_block(
                i, heads, qkv.at[g, 0, here], qkv.at[g, 1], qkv.at[g, 2], go.at[here],
                lse.at[g, here], fence.at[here], sq.at[here], sk,
                grads.at[g, 0, here], dsums.at[g, 0, here],
                dq_scr, dkt, dvt, dskt, later, fsum, qt, dot_,
            )
            hook(g, i)
        grads[g, 1] = dkt[...].T.astype(bf16)
        grads[g, 2] = dvt[...].T.astype(bf16)
        dsums[g, 1] = dskt[...].T

        @pl.when(g == 1)
        def _():
            dsel[:, :HD] = (dsums[0, 0] + dsums[1, 0]).astype(bf16)
            dsel[:, HD:] = (dsums[0, 1] + dsums[1, 1]).astype(bf16)
            sel_mine[...] = mm_tn(dsel[...], normed[...]).astype(bf16)

            @pl.when(odd == 1)
            def _():
                to_core.start()

        def weight_grad(t, _):
            j = 2 - t
            here = pl.ds(pl.multiple_of(j * width, width), width)
            total = mm_tn(grads[g, j], normed[...])

            @pl.when(g == 0)
            def _():
                far_s[here, :] = total.astype(bf16)
                far_copy(j).start()

            @pl.when((g == 1) & (t == 0))
            def _():
                far_copy(2).wait_recv()
                ga[:width, :] = (total + far_r[2 * width :, :].astype(f32)).astype(bf16)
                y_copy(1).start()

                @pl.when(odd == 0)
                def _():
                    to_core.wait_recv()
                    sel_mine[...] = (
                        sel_mine[...].astype(f32) + sel_core[...].astype(f32)
                    ).astype(bf16)

                @pl.when(me == 2)
                def _():
                    to_first.start()

                branch_copy.start()

            @pl.when((g == 1) & (t > 0))
            def _():
                far_copy(j).wait_recv()
                gb[here, :] = (total + far_r[here, :].astype(f32)).astype(bf16)

            return 0

        lax.fori_loop(0, 3, weight_grad, 0)
        return 0

    if gb.shape[0] > 2 * width:
        gb[2 * width :, :] = jnp.zeros((gb.shape[0] - 2 * width, depth), bf16)
        ga[2 * width :, :] = jnp.zeros((ga.shape[0] - 2 * width, depth), bf16)
    lax.fori_loop(0, 2, group, 0)

    @pl.when(me == 0)
    def _():
        to_first.wait_recv()
        both = sel_mine[...].astype(f32) + sel_far[...].astype(f32)
        gb[:HD, :] = (gb[:HD, :].astype(f32) + both[:HD, :]).astype(bf16)
        gb[width : width + HD, :] = (
            gb[width : width + HD, :].astype(f32) + both[HD:, :]
        ).astype(bf16)

    y_copy(0).start()
    forward_early(3)
    fd[block(at, 4), :] = z_finish(4).astype(bf16)
    spread(4)
    y_finish(1)
    need(18, 19, 20, *range(22, LOADS))

    def normed_grad(t, _):
        mine = t // 2
        step = pl.multiple_of(lax.rem(t, 2) * BLK, BLK)
        side = mine * odd + (1 - mine) * (1 - odd)
        part = pl.ds(pl.multiple_of(side * rows + step, BLK), BLK)
        here = pl.ds(step, BLK)
        total = mm(dsel[part, :], sel_w[...])
        for g in range(2):
            for j in range(3):
                total = total + mm(grads[g, j, part, :], w[g, j * width : (j + 1) * width, :])

        @pl.when(mine == 0)
        def _():
            ng_send[here, :] = total.astype(bf16)

        @pl.when(mine == 1)
        def _():
            ng_own[here, :] = total

        @pl.when(t == 1)
        def _():
            core_copy.start()

        return 0

    lax.fori_loop(0, 4, normed_grad, 0)
    z_next(1, 0)
    y_finish(0)
    xhat, r = norm_parts(hidden[...].astype(f32))
    core_copy.wait_recv()
    grad = ng_own[...] + ng_recv[...].astype(f32)
    input_grad[...] = (gmid[...] + norm_back(grad * vecs[5:6, :], xhat, r)).astype(bf16)
    small[...] = jnp.zeros_like(small)
    dgain = jnp.sum(grad * xhat, 0, keepdims=True)
    dshift = jnp.sum(grad, 0, keepdims=True)
    lines = depth // 128
    for j in range(lines):
        small[j : j + 1, :] = dgain[:, j * 128 : (j + 1) * 128]
        small[lines + j : lines + j + 1, :] = dshift[:, j * 128 : (j + 1) * 128]
    for slot, which in ((2, 2), (3, 0), (4, 1), (5, 3)):
        for j in range(lines):
            small[slot * lines + j : slot * lines + j + 1, :] = sums[
                which : which + 1, j * 128 : (j + 1) * 128
            ]
    wide_lines = up_g.shape[1] // 128
    for j in range(wide_lines):
        small[pl.ds(6 * lines + me * wide_lines + j, 1), :] = sums[4:5, j * 128 : (j + 1) * 128]
    base = small_lines(depth, up_g.shape[1]) - 4 * ranks
    for owner, g in ((me, 1), (far, 0)):
        for j, which in enumerate((0, 2)):
            total = jnp.sum(grads[g, which].astype(f32), 0, keepdims=True)
            line = base + 4 * owner + 2 * j
            small[pl.ds(line, 1), :] = total[:, :128]
            small[pl.ds(line + 1, 1), : width - 128] = total[:, 128:]
    total = jnp.sum(dsel[...].astype(f32), 0, keepdims=True)
    lane = lax.broadcasted_iota(jnp.int32, total.shape, 1)
    small[base : base + 1, :] += jnp.where(lane < HD, total, 0.0)
    y_copy(2).start()

    fa[block(at, 1), :] = z_finish(1).astype(bf16)
    spread(1)
    z_next(0, 0)
    y_finish(2)
    forward(3, 0)
    forward_early(4)
    z_next(2, 0)
    forward_early(1)
    fb[block(at, 0), :] = z_finish(0).astype(bf16)
    spread(0)
    forward(4, 0)
    ts[me] = z_finish(2)

    def t_copy(d):
        return plan(ts.at[me], ts.at[me], t_s.at[d], t_r.at[d], tensor=peers[d])

    for d in range(ranks - 1):
        t_copy(d).start()
    for d in range(ranks - 1):
        t_copy(d).wait_recv()
    vec = ts[0]
    for d in range(1, ranks):
        vec = vec + ts[d]
    out_s[block(at, 2), :] = vec
    spread(2)
    forward(1, 0)
    forward_early(0)
    forward_early(2)
    token = odd * rows + lax.broadcasted_iota(jnp.int32, (rows, 1), 0)
    live = jnp.where(token < length, 1.0, 0.0)
    branch_copy.wait_recv()
    output[...] = (live * (partial[...] + bx_recv[...].astype(f32))).astype(bf16)
    forward(0, 0)
    forward(2, 0)
    for k in range(5):
        ay_copy(k, None, 0).wait_recv()
        for b in range(bits):
            for j in stage(b):
                ay_copy(k, b, j).wait_recv()

    @pl.when(odd == 1)
    def _():
        to_core.wait_send()

    @pl.when(me == 2)
    def _():
        to_first.wait_send()

    small_out[...] = out_s[...]
    for c in (far_copy(0), far_copy(1), far_copy(2), out_copy, branch_copy, core_copy):
        c.wait_send()
    for d in range(ranks - 1):
        t_copy(d).wait_send()
    for k in range(5):
        y_copy(k).wait_send()
        ay_copy(k, None, 0).wait_send()
        for b in range(bits):
            for j in stage(b):
                z_copy(k, b, j).wait_send()
                az_copy(k, b, j).wait_send()
                ay_copy(k, b, j).wait_send()


def front_kernel(
    lengths, hidden, out_grad, vecs, qkv, qv_bias, wo,
    *rest,
):
    outs, gcore, gfar, gcross = rest[:18], rest[18], rest[19], rest[20]
    kept = rest[21:39]
    front_body(
        lengths, hidden, out_grad, vecs, qkv, qv_bias, wo, outs, kept, gcore, gfar, gcross, *rest[39:]
    )


def front_body(
    lengths, hidden, out_grad, vecs, qkv, qv_bias, wo, outs, kept, gcore, gfar, gcross,
    out_scr, carry, sel_b, bias2,
    st_s, nm_s, nm_r, gc_s, gc_r, sl_s, sl_r, w_s, w_r, p_s, p_r, e_s, e_r, g_s, g_r, h_s, h_r,
):
    me = lax.axis_index("tensor")
    idx = lax.axis_index("dp")
    odd = lax.rem(me, 2)
    core = me + 1 - 2 * odd
    far = lax.rem(me + 2, 4)
    par = lax.rem(idx, 2)
    ydev = idx + 1 - 2 * par
    rows = hidden.shape[0]
    seq_len = 2 * rows
    width = wo.shape[0]
    heads = width // HD
    (normed, q1, k1, v1, lse1, o1, q2, k2, v2, lse2, o2, fence, sq, sk, w2, wo2, selw, g0) = kept
    stores = []

    def store(*which):
        for j in which:
            copy = pltpu.make_async_copy(kept[j], outs[j], st_s.at[j])
            copy.start()
            stores.append(copy)

    length = jnp.where(me < 2, lengths[0], lengths[1])

    def sel_copies(k, where):
        return [
            pltpu.make_async_remote_copy(
                src_ref=a, dst_ref=a, send_sem=sl_s.at[k, j], recv_sem=sl_r.at[j],
                device_id={"tensor": where}, device_id_type=pl.DeviceIdType.MESH,
            )
            for j, a in enumerate((selw, sel_b))
        ]

    @pl.when(me == 0)
    def _():
        selw[:HD, :] = qkv[:HD, :]
        selw[HD:, :] = qkv[width : width + HD, :]
        sel_b[...] = qv_bias[...]

    meet([{"tensor": core}, {"tensor": far}, {"dp": ydev}])

    @pl.when(me == 0)
    def _():
        for c in sel_copies(0, far) + sel_copies(1, core):
            c.start()

    share = width // 2
    halves = [
        (src, dst, pl.ds(pl.multiple_of(base + par * share, share), share))
        for src, dst, base in (
            (qkv, w2, 0), (qkv, w2, width), (qkv, w2, 2 * width), (wo, wo2, 0)
        )
    ]
    extra = send(qv_bias, bias2, e_s, e_r, tensor=far)
    cross = [
        send(src.at[part], dst.at[part], w_s.at[j], w_r.at[j], tensor=far)
        for j, (src, dst, part) in enumerate(halves)
    ]
    passed = []

    def pass_on(j):
        cross[j].wait_recv()
        _, dst, part = halves[j]
        passed.append(send(dst.at[part], dst.at[part], p_s.at[j], p_r.at[j], dp=ydev))

    spot = pl.multiple_of(odd * rows, rows)
    norm_copies = []
    for c in range(rows // BLK):
        here = pl.ds(c * BLK, BLK)
        there = pl.ds(pl.multiple_of(spot + c * BLK, BLK), BLK)
        xhat, _ = norm_parts(hidden[here, :].astype(f32))
        normed[there, :] = (xhat * vecs[5:6, :] + vecs[6:7, :]).astype(bf16)
        norm_copies.append(
            send(normed.at[there], normed.at[there], nm_s.at[c], nm_r.at[c], tensor=core)
        )
    row = odd * rows + lax.broadcasted_iota(jnp.int32, (rows, 1), 0)
    live = jnp.where(row < length, 1.0, 0.0)
    g0[...] = (out_grad[...].astype(f32) * live).astype(bf16)
    store(17)
    gc = send(g0, gcore, gc_s, gc_r, tensor=core)
    g_parts = [pl.ds(c * BLK, BLK) for c in range(rows // BLK)]
    gf = [
        send(g0.at[p], gfar.at[p], g_s.at[c], g_r.at[c], tensor=far) for c, p in enumerate(g_parts)
    ]

    def project(weight, bias, out):
        def tile(j, _):
            here = pl.ds(pl.multiple_of(j * BLK, BLK), BLK)
            y = mm_nt(normed[here, :], weight)
            if bias is not None:
                y = y + bias
            out[here, :] = y.astype(bf16)
            return 0

        lax.fori_loop(0, seq_len // BLK, tile, 0)

    @pl.when(me == 2)
    def _():
        for c in sel_copies(0, far):
            c.wait_recv()
        for c in sel_copies(1, core):
            c.start()

    for c in norm_copies:
        c.wait_recv()
    store(0)
    project(qkv[:width, :], qv_bias[0:1, :], q1)
    project(qkv[width : 2 * width, :], None, k1)
    project(qkv[2 * width :, :], qv_bias[1:2, :], v1)

    @pl.when(odd == 1)
    def _():
        for c in sel_copies(1, core):
            c.wait_recv()

    store(1, 2, 3)
    def select(j, _):
        here = pl.ds(pl.multiple_of(j * BLK, BLK), BLK)
        y = mm_nt(normed[here, :], selw[...])
        sq[here, :] = (y[:, :HD] + sel_b[0:1, :HD]).astype(bf16)
        sk[here, :] = y[:, HD:].astype(bf16)
        return 0

    lax.fori_loop(0, seq_len // BLK, select, 0)
    store(12, 13, 16)
    carry[...] = jnp.zeros_like(carry)
    pass_on(0)
    for i in range(seq_len // BLK):
        here = pl.ds(i * BLK, BLK)
        make_fence(i, seq_len, length, sq.at[here], sk, fence.at[here], carry)
        fwd_block(
            i, heads, out_scr, q1.at[here], k1, v1, fence.at[here], o1.at[here], lse1.at[here]
        )
        if i < 3:
            pass_on(i + 1)
    store(4, 5, 11)
    extra.wait_recv()
    for j, (out, bias) in enumerate(((q2, bias2[0:1, :]), (k2, None), (v2, bias2[1:2, :]))):
        passed[j].wait_recv()
        project(w2[j * width : (j + 1) * width, :], bias, out)
        store(6 + j)
    store(14)
    gx = []

    def pass_g(c):
        gf[c].wait_recv()
        p = g_parts[c]
        gx.append(send(gfar.at[p], gcross.at[p], h_s.at[c], h_r.at[c], tensor=core))

    for i in range(seq_len // BLK):
        here = pl.ds(i * BLK, BLK)
        fwd_block(
            i, heads, out_scr, q2.at[here], k2, v2, fence.at[here], o2.at[here], lse2.at[here]
        )
    store(9, 10)
    for c in range(rows // BLK):
        pass_g(c)
    gc.wait_recv()
    passed[3].wait_recv()
    store(15)
    for c in gx:
        c.wait_recv()

    @pl.when(me == 0)
    def _():
        for c in sel_copies(0, far):
            c.wait_send()

    @pl.when(odd == 0)
    def _():
        for c in sel_copies(1, core):
            c.wait_send()

    for c in cross + passed + norm_copies + gf + gx + [gc, extra]:
        c.wait_send()
    for c in stores:
        c.wait()


def front(lengths, hidden, out_grad, vecs, qkv, qv_bias, wo):
    rows, depth = hidden.shape
    seq_len, width = 2 * rows, wo.shape[0]
    pieces = rows // BLK
    vmem = pl.BlockSpec(memory_space=pltpu.VMEM)
    dma = pltpu.SemaphoreType.DMA
    heads = jax.ShapeDtypeStruct((seq_len, width), bf16)
    lse = jax.ShapeDtypeStruct((seq_len, 128), f32)
    sel = jax.ShapeDtypeStruct((seq_len, HD), bf16)
    wide = jax.ShapeDtypeStruct((rows, depth), bf16)
    kept = [
        jax.ShapeDtypeStruct((seq_len, depth), bf16),
        heads, heads, heads, lse, heads,
        heads, heads, heads, lse, heads,
        jax.ShapeDtypeStruct((seq_len, seq_len), f32),
        sel, sel,
        jax.ShapeDtypeStruct(qkv.shape, bf16),
        jax.ShapeDtypeStruct(wo.shape, bf16),
        jax.ShapeDtypeStruct((2 * HD, depth), bf16),
        wide,
    ]
    return pl.pallas_call(
        front_kernel,
        in_specs=[pl.BlockSpec(memory_space=pltpu.SMEM)] + [vmem] * 6,
        out_specs=[pl.BlockSpec(memory_space=pl.ANY)] * 21,
        out_shape=kept + [wide, wide, wide],
        scratch_shapes=[pltpu.VMEM(a.shape, a.dtype) for a in kept]
        + [
            pltpu.VMEM((BLK, width), f32),
            pltpu.VMEM((8, seq_len), f32),
            pltpu.VMEM((2, width), f32),
            pltpu.VMEM((2, width), f32),
            dma((18,)),
            dma((pieces,)), dma((pieces,)),
            dma, dma,
            dma((2, 2)), dma((2,)),
            dma((4,)), dma((4,)),
            dma((4,)), dma((4,)),
            dma, dma,
            dma((pieces,)), dma((pieces,)),
            dma((pieces,)), dma((pieces,)),
        ],
        compiler_params=pltpu.CompilerParams(
            collective_id=2, has_side_effects=True, vmem_limit_bytes=60 * 1024 * 1024
        ),
        name="front",
    )(lengths, hidden, out_grad, vecs, qkv, qv_bias, wo)


def small_lines(depth, hidden):
    return (6 * depth + 4 * hidden) // 128 + 16


def go_back(n, set1, set2, fence, sq, sk, rows_in, o1, o2, wo1, wo2, normed, w1, w2, sel_w,
            hidden, vecs, gmid, sums, partial, branch_x, lengths, up_g, down_g):
    m = n // 2
    chunk = up_g.shape[0] // n
    rows, depth = hidden.shape
    piece = -(-small_lines(depth, up_g.shape[1]) // (8 * n)) * 8
    seq_len, width = set1[0].shape
    half, shalf = m * chunk, m * piece
    ranks = 4
    wf = up_g.shape[1]
    small_chunk = -(-2 * width // (16 * n)) * 16
    part_half = m * small_chunk
    vmem = pl.BlockSpec(memory_space=pltpu.VMEM)
    dma = pltpu.SemaphoreType.DMA
    q1, k1, v1, lse1 = set1
    q2, k2, v2, lse2 = set2
    held = (up_g, rows_in, o2, wo2, q2, k2, v2, lse2, fence, sq, sk, normed, down_g, wo1,
            q1, k1, v1, lse1, w2, w1, sel_w, o1, hidden, gmid, vecs, sums, partial)
    anyw = pl.BlockSpec(memory_space=pl.ANY)
    like = lambda a: pltpu.VMEM(a.shape, a.dtype)
    return pl.pallas_call(
        lambda *refs: back_kernel(n, chunk, piece, depth, *refs),
        in_specs=[pl.BlockSpec(memory_space=pltpu.SMEM)] + [anyw] * (LOADS + 3),
        out_specs=[vmem] * 7,
        out_shape=[
            jax.ShapeDtypeStruct((n * chunk, wf), bf16),
            jax.ShapeDtypeStruct((n * chunk, wf), bf16),
            jax.ShapeDtypeStruct((n * small_chunk, depth), bf16),
            jax.ShapeDtypeStruct((n * small_chunk, depth), bf16),
            jax.ShapeDtypeStruct((n * piece, 128), f32),
            jax.ShapeDtypeStruct((rows, depth), bf16),
            jax.ShapeDtypeStruct((rows, depth), bf16),
        ],
        scratch_shapes=[
            pltpu.VMEM((half, wf), bf16), pltpu.VMEM((half, wf), bf16), like(rows_in),
            pltpu.VMEM((2, seq_len, width), bf16),
            pltpu.VMEM((2, width, depth), bf16),
            pltpu.VMEM((2, 3, seq_len, width), bf16),
            pltpu.VMEM((2, seq_len, 128), f32),
            like(fence), like(sq), like(sk), like(normed), pltpu.VMEM((half, wf), bf16),
            pltpu.VMEM((2, 3 * width, depth), bf16),
            like(sel_w), like(hidden), like(gmid), like(vecs), like(sums), like(partial),
            dma((LOADS,)),
            pltpu.VMEM((seq_len, width), bf16),
            pltpu.VMEM((2, 3, seq_len, width), bf16),
            pltpu.VMEM((2, 2, seq_len, HD), f32),
            pltpu.VMEM((BLK, width), f32),
            pltpu.VMEM((width, seq_len), f32),
            pltpu.VMEM((width, seq_len), f32),
            pltpu.VMEM((HD, seq_len), f32),
            pltpu.VMEM((8, seq_len), f32),
            pltpu.VMEM((BLK, seq_len), f32),
            pltpu.VMEM((width, BLK), bf16),
            pltpu.VMEM((width, BLK), bf16),
            pltpu.VMEM((seq_len, 128), bf16),
            pltpu.VMEM((rows, depth), bf16),
            pltpu.VMEM((rows, depth), bf16),
            pltpu.VMEM((rows, depth), f32),
            pltpu.VMEM((3 * width, depth), bf16),
            pltpu.VMEM((3 * width, depth), bf16),
            pltpu.VMEM((width, depth), bf16),
            pltpu.VMEM((width, depth), bf16),
            pltpu.VMEM((n * small_chunk, depth), bf16),
            pltpu.VMEM((n * small_chunk, depth), bf16),
            *[pltpu.VMEM((h, depth), bf16) for h in (half, part_half, part_half)],
            pltpu.VMEM((shalf, 128), f32),
            *[pltpu.VMEM((h, depth), bf16) for h in (half, half, part_half, part_half)],
            pltpu.VMEM((shalf, 128), f32),
            *[
                pltpu.VMEM((m - 1, c, depth), bf16)
                for c in (chunk, chunk, small_chunk, small_chunk)
            ],
            pltpu.VMEM((m - 1, piece, 128), f32),
            pltpu.VMEM((ranks, piece, 128), f32),
            pltpu.VMEM((n * piece, 128), f32),
            pltpu.VMEM((n * piece, 128), f32),
            pltpu.VMEM((rows, depth), bf16),
            *[pltpu.VMEM((2 * HD, depth), bf16)] * 3,
            dma, dma,
            dma((5,)), dma((5,)),
            dma((2,)), dma((2,)),
            dma((5,)), dma((5,)),
            dma((5, m - 1)), dma((5, m - 1)),
            dma((3,)), dma((3,)),
            dma((5, m - 1)), dma((5, m - 1)),
            dma((5, m)), dma((5, m)),
        ],
        compiler_params=pltpu.CompilerParams(
            collective_id=0, has_side_effects=True, vmem_limit_bytes=66_900_000
        ),
        name="go_back",
    )(lengths, up_g, down_g, branch_x, *held)


def shards(
    hidden_in,
    lengths,
    ln1_gain,
    ln1_shift,
    qkv_weight,
    qv_bias,
    out_weight,
    out_bias,
    ln2_gain,
    ln2_shift,
    up_weight,
    up_bias,
    down_weight,
    down_bias,
    out_grad,
):
    n = lax.axis_size("dp")
    ranks = lax.axis_size("tensor")
    me = lax.axis_index("tensor")
    depth = hidden_in.shape[1]
    width = qkv_weight.shape[2]
    hidden = up_bias.shape[0]
    padded = -(-depth // (16 * n)) * 16 * n
    spot = jnp.arange(8)[:, None]
    vecs = jnp.zeros((8, depth), f32)
    for j, vec in enumerate(
        (out_bias, ln2_gain, ln2_shift, down_bias, up_bias.astype(f32), ln1_gain, ln1_shift)
    ):
        vecs = jnp.where(spot == j, vec[None], vecs)
    qkv_rows = jnp.swapaxes(qkv_weight, 1, 2).reshape(3 * width, depth)
    (normed, q1, k1, v1, lse1, o1, q2, k2, v2, lse2, o2, fence, sq, sk, qkv_far, out_far, sel_w,
     *grad_rows) = front(lengths, hidden_in, out_grad, vecs, qkv_rows, qv_bias, out_weight)
    attn_rows, grad_middle, partial, branch_x, up_part, down_part, sums = feed_forward(
        padded, o1, o2, out_weight, out_far, hidden_in, grad_rows, vecs, up_weight, down_weight
    )
    full_u, full_d, full_b, full_a, small, input_grad, output = go_back(
        n, (q1, k1, v1, lse1), (q2, k2, v2, lse2), fence, sq, sk, attn_rows, o1, o2,
        out_weight, out_far, normed, qkv_rows, qkv_far, sel_w, hidden_in, vecs,
        grad_middle, sums, partial, branch_x, lengths, up_part, down_part,
    )
    vectors = small[: 6 * depth // 128].reshape(6, depth)
    lines = (6 * depth + ranks * hidden) // 128
    up_all = small[6 * depth // 128 : lines].reshape(ranks, hidden)
    qv_all = small[lines : lines + 4 * ranks].reshape(ranks, 2, 256)
    up_bias_grad = lax.dynamic_index_in_dim(up_all, me, 0, keepdims=False)
    qv_bias_grad = lax.dynamic_index_in_dim(qv_all, me, 0, keepdims=False)[:, :width]
    qkv_grad = jnp.concatenate([full_b[: 2 * width], full_a[:width]], 0).astype(f32)
    qkv_grad = jnp.swapaxes(qkv_grad.reshape(3, width, depth), 1, 2)
    out_weight_grad = full_a[width : 2 * width].astype(f32)
    return (
        output,
        input_grad,
        vectors[0],
        vectors[1],
        qkv_grad,
        qv_bias_grad,
        out_weight_grad,
        vectors[2],
        vectors[3],
        vectors[4],
        full_u[:depth].astype(f32),
        up_bias_grad,
        full_d[:depth].astype(f32),
        vectors[5],
    )


def solution(mesh):
    return jax.shard_map(
        shards,
        mesh=mesh,
        in_specs=(
            P(("dp", "tensor"), None),
            P("dp"),
            P(),
            P(),
            P(None, None, "tensor"),
            P(None, "tensor"),
            P("tensor", None),
            P(),
            P(),
            P(),
            P(None, "tensor"),
            P("tensor"),
            P("tensor", None),
            P(),
            P(("dp", "tensor"), None),
        ),
        out_specs=(
            P(("dp", "tensor"), None),
            P(("dp", "tensor"), None),
            P(),
            P(),
            P(None, None, "tensor"),
            P(None, "tensor"),
            P("tensor", None),
            P(),
            P(),
            P(),
            P(None, "tensor"),
            P("tensor"),
            P("tensor", None),
            P(),
        ),
        check_vma=False,
    )
```

profile of v0, /device:TPU:0, one launch (start us, length us, event | category | flops | bytes accessed | tf_op | source)
XLA Modules:
  0.0 209.4 jit_solution(3692101603345261426)
XLA Ops:
  0.7 0.7 convert_element_type.17
  1.4 1.5 select_select_fusion.vecs.refs_28_
  2.8 40.6 %front.1 = (bf16[1024,768]{1,0:T(8,128)(2,1)}, bf16[1024,192]{1,0:T(8,128)(2,1)}, bf16[1024,192]{1,0:T(8,128)(2,1)}, bf16[1024,192]{1,0:T(8,128)(2,1)}, f32[1024...) custom-call(s32[2]{0:T(128)} %refs_0_.1, ...), custom_call_target="tpu_custom_call" | custom-call | tf_op jit(solution)/shard_map/front/pallas_call | solution.py:1054
  43.4 50.4 %feed_forward.1 = (bf16[1024,768]{1,0:T(8,128)(2,1)}, f32[512,768]{1,0:T(8,128)}, f32[512,768]{1,0:T(8,128)}, bf16[512,768]{1,0:T(8,128)(2,1)}, bf16[768,768]{1,...) custom-call(bf16[1024,192]{1,0:T(8,128)(2,1)} %get-tuple-element.49.o1.refs_25_, ...), custom_call_target="tpu_custom_call" | custom-call | tf_op jit(solution)/shard_map/feed_forward/pallas_call | solution.py:379
  93.8 104.9 %go_back.1 = (bf16[768,768]{1,0:T(8,128)(2,1)}, bf16[768,768]{1,0:T(8,128)(2,1)}, bf16[384,768]{1,0:T(8,128)(2,1)}, bf16[384,768]{1,0:T(8,128)(2,1)}, f32[128,12...) custom-call(s32[2]{0:T(128)} %refs_0_.1, bf16[768,768]{1,0:T(8,128)(2,1)} %get-tuple-element.56.refs_1_.refs_4_, ...), custom_call_target="tpu_custom_call" | custom-call | tf_op jit(solution)/shard_map/go_back/pallas_call | solution.py:1106
  198.7 0.0 copy-start.4
  198.7 2.0 slice_convert_fusion
  200.7 0.0 copy-done.4
  200.7 0.1 pad_maximum_fusion
  200.8 0.0 copy-start.1
  200.8 1.4 convert_bitcast_fusion
  202.2 0.4 copy-done.1
  202.5 0.0 copy-start
  202.5 1.6 convert_element_type.20
  204.1 0.1 copy-done
  204.2 0.0 copy-start.5
  204.2 0.0 copy-start.3
  204.2 1.6 convert_element_type.21
  205.8 0.0 copy-start.2
  205.8 0.0 copy-done.5
  205.8 0.6 dynamic-slice_reduce_fusion
  206.4 0.6 slice_bitcast_fusion
  207.0 0.6 dynamic-slice_bitcast_fusion
  207.6 0.0 copy-done.3
  207.6 0.9 copy.31
  208.5 0.0 copy-done.2
  208.5 0.9 copy.32
  (8 shorter events, 0.1 us)
Async XLA Ops:
  198.7 2.0 copy-start.4
  200.8 1.7 copy-start.1
  202.5 1.7 copy-start
  204.2 1.6 copy-start.5
  204.2 3.4 %copy-start.3 = (bf16[512,768]{1,0:T(8,128)(2,1)S(1)}, bf16[512,768]{1,0:T(8,128)(2,1)}, u32[]{:S(2)}) copy-start(bf16[512,768]{1,0:T(8,128)(2,1)} %get-tuple-element.112) | copy-start | bytes 2359300
  205.8 2.7 %copy-start.2 = (bf16[512,768]{1,0:T(8,128)(2,1)S(1)}, bf16[512,768]{1,0:T(8,128)(2,1)}, u32[]{:S(2)}) copy-start(bf16[512,768]{1,0:T(8,128)(2,1)} %get-tuple-element.113) | copy-start | bytes 2359300
where the time goes:
time: 210 us; the launch traced here: 209 us
  Pallas kernels  196 us (93%)
  other arithmetic  8.7 us (4%)
  local copies, waits for them, and re-layouts  4.07 us (2%)
    pallas_call x1, Pallas kernels, go_back(): pl.pallas_call(lambda *refs: back_kernel(n, chunk, piece, depth, *refs),...  105 us
    pallas_call x1, Pallas kernels, feed_forward(): pl.pallas_call(feed_kernel, in_specs=[vmem] * 5 + [anyw] * 4 + [vmem] * 3...  50.4 us
    pallas_call x1, Pallas kernels, front(): pl.pallas_call(front_kernel, in_specs=[pl.BlockSpec(memory_space=pltpu.SM...  40.6 us

commit v1 on v0

--- a/solution.py
+++ b/solution.py
@@ -584,27 +584,33 @@
     to_first = plan(sel_mine, sel_far, sl_s.at[1], sl_r.at[1], tensor=far)
 
     y_copy(3).start()
-    y_copy(4).start()
     need(*range(13))
 
     def hook(g, i):
-        if i == 1:
+        if i == 0:
 
             @pl.when(g == 0)
             def _():
                 y_finish(3)
+                y_copy(4).start()
+
+        if i == 1:
 
             @pl.when(g == 1)
             def _():
                 fu[block(at, 3), :] = z_finish(3).astype(bf16)
                 spread(3)
-                z_next(4, 0)
 
         if i == seq_len // BLK - 1:
 
             @pl.when(g == 1)
             def _():
                 z_next(3, 0)
+
+        if i == 2:
+
+            @pl.when(g == 1)
+            def _():
                 y_finish(4)
 
     def group(g, _):
@@ -709,6 +715,7 @@
         ).astype(bf16)
 
     y_copy(0).start()
+    z_next(4, 0)
     forward_early(3)
     fd[block(at, 4), :] = z_finish(4).astype(bf16)
     spread(4)

time: 210 us -> 206 us (0.981)
  Pallas kernels: 196 us -> 192 us
    pallas_call x1, Pallas kernels: 105 us -> 101 us  [go_back(): pl.pallas_call(lambda *refs: back_kernel(n, chunk, piece, depth, *refs),...]
where the time goes in v1:
time: 206 us
  Pallas kernels  192 us (93%)
  other arithmetic  8.7 us (4%)
  local copies, waits for them, and re-layouts  4.07 us (2%)
    pallas_call x1, Pallas kernels, go_back(): pl.pallas_call(lambda *refs: back_kernel(n, chunk, piece, depth, *refs),...  101 us
    pallas_call x1, Pallas kernels, feed_forward(): pl.pallas_call(feed_kernel, in_specs=[vmem] * 5 + [anyw] * 4 + [vmem] * 3...  50.4 us
    pallas_call x1, Pallas kernels, front(): pl.pallas_call(front_kernel, in_specs=[pl.BlockSpec(memory_space=pltpu.SM...  40.6 us

profile of v1, /device:TPU:0, one launch (start us, length us, event | category | flops | bytes accessed | tf_op | source)
XLA Modules:
  0.0 205.7 jit_solution(14136217282748631535)
XLA Ops:
  0.7 0.7 convert_element_type.17
  1.4 1.5 select_select_fusion.vecs.refs_28_
  2.8 40.6 %front.1 = (bf16[1024,768]{1,0:T(8,128)(2,1)}, bf16[1024,192]{1,0:T(8,128)(2,1)}, bf16[1024,192]{1,0:T(8,128)(2,1)}, bf16[1024,192]{1,0:T(8,128)(2,1)}, f32[1024...) custom-call(s32[2]{0:T(128)} %refs_0_.1, ...), custom_call_target="tpu_custom_call" | custom-call | tf_op jit(solution)/shard_map/front/pallas_call | solution.py:1061
  43.4 50.4 %feed_forward.1 = (bf16[1024,768]{1,0:T(8,128)(2,1)}, f32[512,768]{1,0:T(8,128)}, f32[512,768]{1,0:T(8,128)}, bf16[512,768]{1,0:T(8,128)(2,1)}, bf16[768,768]{1,...) custom-call(bf16[1024,192]{1,0:T(8,128)(2,1)} %get-tuple-element.49.o1.refs_25_, ...), custom_call_target="tpu_custom_call" | custom-call | tf_op jit(solution)/shard_map/feed_forward/pallas_call | solution.py:379
  93.8 101.2 %go_back.1 = (bf16[768,768]{1,0:T(8,128)(2,1)}, bf16[768,768]{1,0:T(8,128)(2,1)}, bf16[384,768]{1,0:T(8,128)(2,1)}, bf16[384,768]{1,0:T(8,128)(2,1)}, f32[128,12...) custom-call(s32[2]{0:T(128)} %refs_0_.1, bf16[768,768]{1,0:T(8,128)(2,1)} %get-tuple-element.56.refs_1_.refs_4_, ...), custom_call_target="tpu_custom_call" | custom-call | tf_op jit(solution)/shard_map/go_back/pallas_call | solution.py:1113
  195.1 0.0 copy-start.4
  195.1 2.0 slice_convert_fusion
  197.1 0.0 copy-done.4
  197.1 0.1 pad_maximum_fusion
  197.1 0.0 copy-start.1
  197.1 1.4 convert_bitcast_fusion
  198.5 0.4 copy-done.1
  198.8 0.0 copy-start
  198.9 1.6 convert_element_type.20
  200.4 0.1 copy-done
  200.5 0.0 copy-start.5
  200.5 0.0 copy-start.3
  200.5 1.6 convert_element_type.21
  202.1 0.0 copy-start.2
  202.1 0.0 copy-done.5
  202.1 0.6 dynamic-slice_reduce_fusion
  202.7 0.6 slice_bitcast_fusion
  203.4 0.6 dynamic-slice_bitcast_fusion
  204.0 0.0 copy-done.3
  204.0 0.9 copy.31
  204.8 0.0 copy-done.2
  204.8 0.9 copy.32
  (8 shorter events, 0.1 us)
Async XLA Ops:
  195.1 2.0 copy-start.4
  197.1 1.7 copy-start.1
  198.8 1.7 copy-start
  200.5 1.6 copy-start.5
  200.5 3.4 %copy-start.3 = (bf16[512,768]{1,0:T(8,128)(2,1)S(1)}, bf16[512,768]{1,0:T(8,128)(2,1)}, u32[]{:S(2)}) copy-start(bf16[512,768]{1,0:T(8,128)(2,1)} %get-tuple-element.112) | copy-start | bytes 2359300
  202.1 2.7 %copy-start.2 = (bf16[512,768]{1,0:T(8,128)(2,1)S(1)}, bf16[512,768]{1,0:T(8,128)(2,1)}, u32[]{:S(2)}) copy-start(bf16[512,768]{1,0:T(8,128)(2,1)} %get-tuple-element.113) | copy-start | bytes 2359300
